TPU v7x, 32 devices: a whole 2x2x4 slice. The times are simulated.
32 devices in a mesh: chan: 4 (over z), pulse: 4 (over x, core), range: 2 (over y).
Axes of the slice: x: 2, y: 2, z: 4, core: 2. Of those that a mesh axis runs over, the one named last changes fastest.
Arguments:
- signal: bfloat16 [2, 64, 32, 8192], P(None, 'chan', 'pulse', 'range'), may hold values from -6 to 6
- steering: bfloat16 [2, 32, 64], replicated, may hold values from -0.5 to 0.5
- spectrum: float32 [2, 8192], replicated, may hold values from -6 to 6
Outputs:
- detection: float32 [32, 32, 8192], P('chan', 'pulse', 'range')
All inputs are finite; a program needn't handle non-finite values.
Results may differ from a plain program's by a relative error of at most 0.0087.
Values may be sent and summed in bfloat16 or wider, within the bound.
A program may use at most 64 MiB of HBM per device.

v0:
```python
import math
import jax
import jax.numpy as jnp
from jax import lax
from jax.sharding import PartitionSpec as P

GUARD = 4
TRAIN = 16
PRECISE = lax.Precision.HIGHEST
NOISE_FLOOR = 0.25


def padded_2(x, sides, width):
    for axis, dim in sides:
        peers, length = (lax.axis_size(axis), x.shape[dim])
        up = [(i, (i + 1) % peers) for i in range(peers - 1)]
        down = [(j, i) for i, j in up]
        last = lax.slice_in_dim(x, length - width, length, axis=dim)
        initial = lax.slice_in_dim(x, 0, width, axis=dim)
        before = lax.ppermute(last, axis, up)
        after = lax.ppermute(initial, axis, down)
        x = jnp.concatenate([before, x, after], axis=dim)
    return x


def doppler_tables(pulse_count):
    row_ids = lax.broadcasted_iota(jnp.int32, (pulse_count, pulse_count), 0)
    col_ids = lax.broadcasted_iota(jnp.int32, (pulse_count, pulse_count), 1)
    phase_angle = (row_ids * col_ids % pulse_count).astype(jnp.float32) * (
        2.0 * math.pi / pulse_count
    )
    norm_scale = 1.0 / math.sqrt(pulse_count)
    table_real = (jnp.cos(phase_angle) * norm_scale).astype(jnp.bfloat16)
    table_imag = (-jnp.sin(phase_angle) * norm_scale).astype(jnp.bfloat16)
    return (table_real, table_imag)


def phase_table(row_count, col_count, period_len, direction):
    row_ids = lax.broadcasted_iota(jnp.int32, (row_count, col_count), 0)
    col_ids = lax.broadcasted_iota(jnp.int32, (row_count, col_count), 1)
    phase_angle = (row_ids * col_ids % period_len).astype(jnp.float32) * (
        2.0 * math.pi / period_len
    )
    return (jnp.cos(phase_angle), direction * jnp.sin(phase_angle))


def rotate_by(field_pair, table_pair):
    return (
        field_pair[0] * table_pair[0] - field_pair[1] * table_pair[1],
        field_pair[0] * table_pair[1] + field_pair[1] * table_pair[0],
    )


def mix_blocks(table_pair, field_pair):

    def contract(table_part, field_part):
        return jnp.einsum("km,bpmn->bpkn", table_part, field_part, precision=PRECISE)

    return (
        contract(table_pair[0], field_pair[0]) - contract(table_pair[1], field_pair[1]),
        contract(table_pair[0], field_pair[1]) + contract(table_pair[1], field_pair[0]),
    )


def mix_lanes(field_pair, table_pair):

    def contract(field_part, table_part):
        return jnp.einsum("bpkm,mn->bpkn", field_part, table_part, precision=PRECISE)

    return (
        contract(field_pair[0], table_pair[0]) - contract(field_pair[1], table_pair[1]),
        contract(field_pair[0], table_pair[1]) + contract(field_pair[1], table_pair[0]),
    )


def local_transform(field_pair, direction):
    size_all = field_pair[0].shape[-1]
    blocks = size_all // 128
    leading = field_pair[0].shape[:-1]
    shaped = tuple((member.reshape(leading + (blocks, 128)) for member in field_pair))
    outer_table = phase_table(blocks, blocks, blocks, direction)
    twiddle = phase_table(blocks, 128, size_all, direction)
    inner_table = phase_table(128, 128, 128, direction)
    if direction < 0:
        shaped = mix_blocks(outer_table, shaped)
        shaped = rotate_by(shaped, twiddle)
        shaped = mix_lanes(shaped, inner_table)
    else:
        shaped = mix_lanes(shaped, inner_table)
        shaped = rotate_by(shaped, twiddle)
        shaped = mix_blocks(outer_table, shaped)
    return tuple((member.reshape(leading + (size_all,)) for member in shaped))


def stack_weights(w_real, w_imag):
    return jnp.concatenate(
        [jnp.concatenate([w_real, -w_imag], 1), jnp.concatenate([w_imag, w_real], 1)], 0
    )


def shards(signal, steering, spectrum):
    beam_count = steering.shape[1]
    chan_count = steering.shape[2]
    pulse_local = signal.shape[2]
    gate_count = signal.shape[3]
    stacked = stack_weights(steering[0], steering[1])
    samples = lax.all_to_all(signal, "chan", split_axis=2, concat_axis=1, tiled=True)
    pulses_here = samples.shape[2]
    gates_here = samples.shape[3]
    flat_samples = samples.reshape(2 * chan_count, pulses_here * gates_here)
    formed = jnp.dot(stacked, flat_samples, preferred_element_type=jnp.float32)
    formed = formed.astype(jnp.bfloat16).reshape(2, beam_count, pulses_here, gates_here)
    beam_data = lax.all_to_all(formed, "chan", split_axis=1, concat_axis=2, tiled=True)
    beam_local = beam_data.shape[1]
    range_count = lax.axis_size("range")
    range_index = lax.axis_index("range")
    full_length = gate_count * range_count
    inverse_scale = 1.0 / full_length
    shard_piece = lax.all_gather(beam_data, "range", axis=3, tiled=True)
    shard_count = shard_piece.shape[3] // gate_count
    members = shard_piece.astype(jnp.float32).reshape(
        2, beam_local, pulse_local, shard_count, gate_count
    )
    source = jnp.arange(shard_count, dtype=jnp.int32)
    phase_angle = (source * range_index % range_count).astype(jnp.float32) * (
        2.0 * math.pi / range_count
    )
    cos_part = jnp.cos(phase_angle)[:, None]
    sin_part = -jnp.sin(phase_angle)[:, None]
    sum_real = jnp.sum(members[0] * cos_part - members[1] * sin_part, axis=2)
    sum_imag = jnp.sum(members[0] * sin_part + members[1] * cos_part, axis=2)
    folded = (sum_real, sum_imag)
    gate_ids = lax.broadcasted_iota(jnp.int32, (gate_count,), 0)
    global_angle = (gate_ids * range_index % full_length).astype(jnp.float32) * (
        2.0 * math.pi / full_length
    )
    folded = rotate_by(folded, (jnp.cos(global_angle), -jnp.sin(global_angle)))
    spectrum_local = local_transform(folded, -1.0)
    response = spectrum.reshape(2, gate_count, range_count)
    response = lax.dynamic_index_in_dim(response, range_index, axis=2, keepdims=False)
    response = jnp.transpose(response.reshape(2, 128, gate_count // 128), (0, 2, 1)).reshape(
        2, gate_count
    )
    filtered = rotate_by(spectrum_local, (response[0], response[1]))
    restored = local_transform(filtered, 1.0)
    restored = rotate_by(restored, (jnp.cos(global_angle), jnp.sin(global_angle)))
    shard_piece = (
        lax.all_gather(restored[0], "range", axis=2, tiled=True),
        lax.all_gather(restored[1], "range", axis=2, tiled=True),
    )
    shard_count = shard_piece[0].shape[2] // gate_count
    rows_real = shard_piece[0].reshape(beam_local, pulse_local, shard_count, gate_count)
    rows_imag = shard_piece[1].reshape(beam_local, pulse_local, shard_count, gate_count)
    source = jnp.arange(shard_count, dtype=jnp.int32)
    phase_angle = (source * range_index % range_count).astype(jnp.float32) * (
        2.0 * math.pi / range_count
    )
    cos_part = jnp.cos(phase_angle)[:, None]
    sin_part = jnp.sin(phase_angle)[:, None]
    sum_real = jnp.sum(rows_real * cos_part - rows_imag * sin_part, axis=2)
    sum_imag = jnp.sum(rows_real * sin_part + rows_imag * cos_part, axis=2)
    compressed = jnp.stack([sum_real * inverse_scale, sum_imag * inverse_scale]).astype(
        jnp.bfloat16
    )
    pulse_total = pulse_local * lax.axis_size("pulse")
    dop_real, dop_imag = doppler_tables(pulse_total)
    columns = lax.all_to_all(compressed, "pulse", split_axis=3, concat_axis=2, tiled=True)

    def product(table_part, values):
        return jnp.einsum("fp,bpr->bfr", table_part, values, preferred_element_type=jnp.float32)

    mixed_real = product(dop_real, columns[0]) - product(dop_imag, columns[1])
    mixed_imag = product(dop_real, columns[1]) + product(dop_imag, columns[0])
    power_part = lax.all_to_all(
        mixed_real * mixed_real + mixed_imag * mixed_imag,
        "pulse",
        split_axis=1,
        concat_axis=2,
        tiled=True,
    )
    halo_width = GUARD + TRAIN
    padded = padded_2(power_part, (("range", 2),), halo_width)
    window_sum = jnp.zeros_like(power_part)
    for offset in range(1, TRAIN + 1):
        left_start = halo_width - GUARD - offset
        right_start = halo_width + GUARD + offset
        window_sum = (
            window_sum
            + padded[:, :, left_start : left_start + gate_count]
            + padded[:, :, right_start : right_start + gate_count]
        )
    noise_level = window_sum / (2.0 * TRAIN)
    return power_part / (noise_level + NOISE_FLOOR)


def solution(mesh):
    in_specs = (P(None, "chan", "pulse", "range"), P(), P())
    out_specs = P("chan", "pulse", "range")
    return jax.shard_map(shards, mesh=mesh, in_specs=in_specs, out_specs=out_specs, check_vma=False)
```

profile of v0, /device:TPU:0, one launch (start us, length us, event | category | flops | bytes accessed | tf_op | source)
XLA Modules:
  0.0 388.4 jit_solution(4963313028370823325)
XLA Ops:
  6.5 4.1 %copy.81 = bf16[2,16,8,4096]{3,1,0,2:T(8,128)(2,1)} copy(bf16[2,16,8,4096]{3,2,1,0:T(8,128)(2,1)} %param.3) | data formatting | bytes 4194304 | tf_op args[0]
  10.6 6.5 %all-to-all-start = ((bf16[2,16,8,4096]{3,1,0,2:T(8,128)(2,1)}), bf16[2,16,8,4096]{3,1,0,2:T(8,128)(2,1)S(1)}, u32[]{:S(2)}, u32[]{:S(2)}) async-start(bf16[2,16,8,4096]{3,1,0,2:T(8,128)(2,1)} %copy.81), calls=%async_computation | async-start | bytes 4194304 | tf_op jit(solution)/shard_map/all_to_all | solution.py:107
  17.1 48.2 %all-to-all-done = bf16[2,16,8,4096]{3,1,0,2:T(8,128)(2,1)S(1)} async-done(((bf16[2,16,8,4096]{3,1,0,2:T(8,128)(2,1)}), bf16[2,16,8,4096]{3,1,0,2:T(8,128)(2,1)S(1)}, u32[]{:S(2)}, u32[]{:S(2)}) %all-to-all-start) | async-done | bytes 2097184 | tf_op jit(solution)/shard_map/all_to_all | solution.py:107
  65.3 2.2 copy.82
  71.0 27.7 %all_to_all.66 = bf16[2,32,2,4096]{3,2,0,1:T(2,128)(2,1)S(1)} all-to-all(bf16[2,32,2,4096]{3,2,0,1:T(2,128)(2,1)S(1)} %copy.83), channel_id=1, replica_groups=mesh['chan'=4,'pulse'=4,'range'=2] {'chan'}, dimensions={1} | all-to-all | bytes 2097152 | tf_op jit(solution)/shard_map/all_to_all | solution.py:113
  100.6 6.4 %reshape.188 = f32[2,4096,2]{2,1,0:T(8,128)} reshape(f32[2,8192]{1,0:T(2,128)S(1)} %copy-done.1) | data formatting | bytes 131072 | tf_op jit(solution)/shard_map/reshape | solution.py:139
  107.0 4.7 %dynamic-slice_reduce_fusion = f32[2,4096]{1,0:T(2,128)S(1)} fusion(f32[2,4096,2]{2,1,0:T(8,128)} %reshape.188, s32[]{:T(128)S(6)} %select_n.134), kind=kLoop, calls=%fused_computation.31 | loop fusion | bytes 65540 | tf_op jit(solution)/shard_map/jit(dynamic_index_in_dim)/dynamic_slice | solution.py:140
  112.5 20.2 %all-gather.4.cloned.1.call-done = bf16[2,8,8,8192]{3,1,2,0:T(8,128)(2,1)} async-done(((bf16[2,8,8,4096]{3,1,2,0:T(8,128)(2,1)}), bf16[2,8,8,8192]{3,1,2,0:T(8,128)(2,1)}) %all-gather.4.cloned.1.call-update) | async-done | bytes 2097168 | tf_op jit(solution)/shard_map/all_gather | solution.py:119
  132.7 3.9 %fusion.271 = (f32[1,8,8,8192]{3,1,2,0:T(8,128)}, f32[1,8,8,8192]{3,1,2,0:T(8,128)}) fusion(bf16[2,8,8,8192]{3,1,2,0:T(8,128)(2,1)} %all-gather.4.cloned.1.call-done), kind=kLoop, calls=%fused_computation.365 | loop fusion | bytes 8388608 | tf_op jit(solution)/shard_map/slice | solution.py:130
  136.6 3.0 reshape.202
  139.7 4.4 %reshape.203 = f32[8,8,2,4096]{3,2,0,1:T(2,128)} reshape(f32[1,8,8,8192]{3,1,2,0:T(8,128)} %get-tuple-element.12) | data formatting | bytes 4194304 | tf_op jit(solution)/shard_map/squeeze | solution.py:130
  144.1 5.8 %subtract_reduce_fusion.1 = (f32[8,8,4096]{2,1,0:T(8,128)S(1)}, f32[8,8,4096]{2,1,0:T(8,128)S(1)}) fusion(f32[8,8,2,4096]{3,2,0,1:T(2,128)} %reshape.203, f32[8,8,2,4096]{3,2,0,1:T(2,128)S(1)} %reshape.202, f32[2]{0:T(128)S(1)} %get-tuple-element.24, f32[2]{0:T(128)S(1)} %get-tuple-element.23), kind=kLoop, calls=%fused_computation.35 | loop fusion | flops 3670016 | bytes 6291472 | tf_op jit(solution)/shard_map/reduce_sum | solution.py:130
  152.6 1.5 fusion.84
  154.1 1.5 fusion.2
  155.6 1.5 fusion.3
  169.8 2.2 fusion
  172.0 2.4 reshape.191
  174.3 2.2 fusion.1
  176.5 1.5 reshape.190
  178.1 1.6 multiply_subtract_fusion
  180.4 32.5 %all-gather.6.cloned.1.call-done = f32[8,8,8192]{2,1,0:T(8,128)} async-done(((f32[8,8,4096]{2,1,0:T(8,128)}), f32[8,8,8192]{2,1,0:T(8,128)}) %all-gather.6.cloned.1.call-update) | async-done | bytes 2097168 | tf_op jit(solution)/shard_map/all_gather | solution.py:148
  212.9 34.7 %all-gather.8.cloned.1.call-done = f32[8,8,8192]{2,1,0:T(8,128)} async-done(((f32[8,8,4096]{2,1,0:T(8,128)}), f32[8,8,8192]{2,1,0:T(8,128)}) %all-gather.8.cloned.1.call-update) | async-done | bytes 2097168 | tf_op jit(solution)/shard_map/all_gather | solution.py:149
  247.6 3.2 subtract_reduce_fusion
  252.1 14.0 %copy.106 = bf16[2,8,8,4096]{2,1,0,3:T(8,128)(2,1)} copy(bf16[2,8,8,4096]{3,1,2,0:T(8,128)(2,1)S(1)} %pad_maximum_fusion.2) | data formatting | bytes 2097152 | tf_op jit(solution)/shard_map/stack | solution.py:162
  266.1 20.5 %reshape.205 = bf16[4,2,65536]{2,1,0:T(2,128)(2,1)S(1)} reshape(bf16[4096,2,8,8]{3,2,1,0:T(8,128)(2,1)} %bitcast.133) | data formatting | bytes 2097152
  286.6 17.2 %all_to_all.67 = bf16[4,2,65536]{2,1,0:T(2,128)(2,1)S(1)} all-to-all(bf16[4,2,65536]{2,1,0:T(2,128)(2,1)S(1)} %reshape.205), channel_id=1, replica_groups=mesh['chan'=4,'pulse'=4,'range'=2] {'pulse'}, dimensions={0} | all-to-all | bytes 2097152 | tf_op jit(solution)/shard_map/all_to_all | solution.py:167
  303.8 21.7 %reshape.206 = bf16[4096,2,8,8]{3,2,1,0:T(8,128)(2,1)} reshape(bf16[4,2,65536]{2,1,0:T(2,128)(2,1)S(1)} %all_to_all.67) | data formatting | bytes 2097152
  325.5 16.0 %copy.107 = bf16[2,8,8,4,1024]{4,2,3,1,0:T(8,128)(2,1)S(1)} copy(bf16[2,8,8,4,1024]{2,1,0,4,3:T(8,128)(2,1)} %bitcast.134) | data formatting | bytes 2097152 | tf_op jit(solution)/shard_map/all_to_all | solution.py:167
  343.6 16.9 %all_to_all.68 = f32[8,32,1024]{2,0,1:T(8,128)S(1)} all-to-all(f32[8,32,1024]{2,0,1:T(8,128)S(1)} %copy.108), channel_id=1, replica_groups=mesh['chan'=4,'pulse'=4,'range'=2] {'pulse'}, dimensions={1} | all-to-all | bytes 2097152 | tf_op jit(solution)/shard_map/all_to_all | solution.py:174
  361.2 2.4 collective-permute-start
  365.2 4.2 %collective-permute-done.1 = f32[8,8,20]{2,1,0:T(8,128)S(1)} collective-permute-done((f32[8,8,20]{2,1,0:T(8,128)S(1)}, f32[8,8,20]{2,1,0:T(8,128)S(1)}, u32[]{:S(2)}, u32[]{:S(2)}) %collective-permute-start.1) | collective-permute-done | bytes 5152 | tf_op jit(solution)/shard_map/ppermute | solution.py:21
  369.4 12.0 %fusion.14 = f32[8,8,4096]{2,1,0:T(8,128)} fusion(f32[8,8,4096]{2,1,0:T(8,128)S(1)} %bitcast.151, f32[8,8,20]{2,1,0:T(8,128)S(1)} %collective-permute-done.1, f32[8,8,20]{2,1,0:T(8,128)S(1)} %collective-permute-done), kind=kLoop, calls=%fused_computation.60 | loop fusion | flops 17301504 | bytes 2107392 | tf_op jit(solution)/shard_map/div | solution.py:193
  (55 shorter events, 27.8 us)
Async XLA Ops:
  10.6 6.5 %copy-start.2 = (bf16[2,32,64]{2,1,0:T(8,128)(2,1)S(1)}, bf16[2,32,64]{2,1,0:T(8,128)(2,1)}, u32[]{:S(2)}) copy-start(bf16[2,32,64]{2,1,0:T(8,128)(2,1)} %param.4) | copy-start | bytes 24580
  10.6 54.7 %all-to-all-start = ((bf16[2,16,8,4096]{3,1,0,2:T(8,128)(2,1)}), bf16[2,16,8,4096]{3,1,0,2:T(8,128)(2,1)S(1)}, u32[]{:S(2)}, u32[]{:S(2)}) async-start(bf16[2,16,8,4096]{3,1,0,2:T(8,128)(2,1)} %copy.81), calls=%async_computation | async-start | bytes 4194304 | tf_op jit(solution)/shard_map/all_to_all | solution.py:107
  17.1 115.6 %all-gather.4.cloned.1.call-start = ((), (), s32[]{:S(2)}) async-start(), calls=%async_computation.4 | async-start | bytes 3145728 | tf_op jit(solution)/shard_map/all_gather | solution.py:119
  99.3 1.3 copy-start.1
  100.4 112.5 %all-gather.6.cloned.1.call-start = ((), (), s32[]{:S(2)}) async-start(), calls=%async_computation.5 | async-start | bytes 3145728 | tf_op jit(solution)/shard_map/all_gather | solution.py:148
  176.5 1.5 copy-start
  179.7 67.9 %all-gather.8.cloned.1.call-start = ((), (), s32[]{:S(2)}) async-start(), calls=%async_computation.6 | async-start | bytes 3145728 | tf_op jit(solution)/shard_map/all_gather | solution.py:149
  361.2 4.0 %collective-permute-start = (f32[8,8,20]{2,1,0:T(8,128)S(1)}, f32[8,8,20]{2,1,0:T(8,128)S(1)}, u32[]{:S(2)}, u32[]{:S(2)}) collective-permute-start(f32[8,8,20]{2,1,0:T(8,128)S(1)} %get-tuple-element.13), channel_id=1, source_target_pairs={{0,1},{2,3},{4,5},{6,7},{8,9},{10,11},{12,13},{14,15},{16,17},{18,... | collective-permute-start | bytes 15368 | tf_op jit(solution)/shard_map/ppermute | solution.py:20
  363.6 5.8 %collective-permute-start.1 = (f32[8,8,20]{2,1,0:T(8,128)S(1)}, f32[8,8,20]{2,1,0:T(8,128)S(1)}, u32[]{:S(2)}, u32[]{:S(2)}) collective-permute-start(f32[8,8,20]{2,1,0:T(8,128)S(1)} %get-tuple-element.14), channel_id=1, source_target_pairs={{1,0},{3,2},{5,4},{7,6},{9,8},{11,10},{13,12},{15,14},{17,16},{19,... | collective-permute-start | bytes 15368 | tf_op jit(solution)/shard_map/ppermute | solution.py:21
Sparse Core Ops, SparseCore 0:
  100.5 32.1 all-gather.3
  179.8 33.0 all-gather.5
  214.5 33.0 all-gather.7
where the time goes:
time: 395 us; the launch traced here: 388 us
  waiting for transfers between devices  141 us (36%)
  local copies, waits for them, and re-layouts  112 us (28%)
  blocking collectives  61.8 us (16%)
  matrix products  24.9 us (6%)
  other arithmetic  24.3 us (6%)
  between operations  13.9 us (4%)
  starting transfers between devices  10.5 us (3%)
    unnamed x12, local copies, waits for them, and re-layouts  48.9 us
    all_to_all x1, waiting for transfers between devices, shards(): lax.all_to_all(signal, 'chan', split_axis=2, concat_axis=1, tiled=True)  48.2 us
    all_gather x1, waiting for transfers between devices, shards(): lax.all_gather(restored[1], 'range', axis=2, tiled=True)  34.7 us
    all_gather x1, waiting for transfers between devices, shards(): lax.all_gather(restored[0], 'range', axis=2, tiled=True)  32.5 us
    all_to_all x1, blocking collectives, shards(): lax.all_to_all(formed, 'chan', split_axis=1, concat_axis=2, tiled=True)  27.7 us
    all_gather x1, waiting for transfers between devices, shards(): shard_piece = lax.all_gather(beam_data, 'range', axis=3, tiled=True)  20.2 us
    all_to_all x1, blocking collectives, shards(): lax.all_to_all(compressed, 'pulse', split_axis=3, concat_axis=2, tiled=True)  17.2 us
    all_to_all x1, blocking collectives, shards(): lax.all_to_all(mixed_real * mixed_real + mixed_imag * mixed_imag, 'pulse'...  16.9 us
  transfers between devices with their start and end apart: 6, of which 6 were waited for; matrix products, arithmetic and copies ran while one was open for 3% of the time, Pallas kernels for 0%

commit v1 on v0

--- a/solution.py
+++ b/solution.py
@@ -164,7 +164,12 @@
     )
     pulse_total = pulse_local * lax.axis_size("pulse")
     dop_real, dop_imag = doppler_tables(pulse_total)
-    columns = lax.all_to_all(compressed, "pulse", split_axis=3, concat_axis=2, tiled=True)
+    columns = jnp.concatenate(
+        lax.all_to_all(
+            jnp.stack(jnp.split(compressed, lax.axis_size("pulse"), axis=3)), "pulse", 0, 0
+        ),
+        axis=2,
+    )
 
     def product(table_part, values):
         return jnp.einsum("fp,bpr->bfr", table_part, values, preferred_element_type=jnp.float32)

time: 395 us -> 323 us (0.82)
  local copies, waits for them, and re-layouts: 112 us -> 40.5 us
    unnamed x12 -> x10, local copies, waits for them, and re-layouts: 48.9 us -> 6.64 us
    all_to_all x1 -> x0, local copies, waits for them, and re-layouts: 16 us -> none  [shards(): lax.all_to_all(compressed, 'pulse', split_axis=3, concat_axis=2, tiled=True)]
    another operation x1, local copies, waits for them, and re-layouts: 14 us -> 0.6 us  [shards(): jnp.stack(jnp.split(compressed, lax.axis_size('pulse'), axis=3))]
  transfers between devices with their start and end apart: 6 -> 6, of which waited for: 6 -> 6; matrix products, arithmetic and copies ran while one was open for 3% -> 4% of each run, Pallas kernels for 0% -> 0%
where the time goes in v1:
time: 323 us; the launch traced here: 317 us
  waiting for transfers between devices  141 us (44%)
  blocking collectives  61.5 us (19%)
  local copies, waits for them, and re-layouts  40.5 us (13%)
  matrix products  25.1 us (8%)
  other arithmetic  24.6 us (8%)
  between operations  13.7 us (4%)
  starting transfers between devices  10.4 us (3%)
    all_to_all x1, waiting for transfers between devices, shards(): lax.all_to_all(signal, 'chan', split_axis=2, concat_axis=1, tiled=True)  48.2 us
    all_gather x1, waiting for transfers between devices, shards(): lax.all_gather(restored[1], 'range', axis=2, tiled=True)  34.7 us
    all_gather x1, waiting for transfers between devices, shards(): lax.all_gather(restored[0], 'range', axis=2, tiled=True)  32.5 us
    all_to_all x1, blocking collectives, shards(): lax.all_to_all(formed, 'chan', split_axis=1, concat_axis=2, tiled=True)  27.7 us
    all_gather x1, waiting for transfers between devices, shards(): shard_piece = lax.all_gather(beam_data, 'range', axis=3, tiled=True)  20.3 us
    all_to_all x1, blocking collectives, shards(): lax.all_to_all(jnp.stack(jnp.split(compressed, lax.axis_size('pulse'), ax...  17 us
    all_to_all x1, blocking collectives, shards(): lax.all_to_all(mixed_real * mixed_real + mixed_imag * mixed_imag, 'pulse'...  16.9 us
    dot_general x8, matrix products, contract(): jnp.einsum('km,bpmn->bpkn', table_part, field_part, precision=PRECISE)  12.9 us
  transfers between devices with their start and end apart: 6, of which 6 were waited for; matrix products, arithmetic and copies ran while one was open for 4% of the time, Pallas kernels for 0%

profile of v1, /device:TPU:0, one launch (start us, length us, event | category | flops | bytes accessed | tf_op | source)
XLA Modules:
  0.0 316.7 jit_solution(8438806571566218374)
XLA Ops:
  6.5 4.1 %copy.93 = bf16[2,16,8,4096]{3,1,0,2:T(8,128)(2,1)} copy(bf16[2,16,8,4096]{3,2,1,0:T(8,128)(2,1)} %param.3) | data formatting | bytes 4194304 | tf_op args[0]
  10.6 6.5 %all-to-all-start = ((bf16[2,16,8,4096]{3,1,0,2:T(8,128)(2,1)}), bf16[2,16,8,4096]{3,1,0,2:T(8,128)(2,1)S(1)}, u32[]{:S(2)}, u32[]{:S(2)}) async-start(bf16[2,16,8,4096]{3,1,0,2:T(8,128)(2,1)} %copy.93), calls=%async_computation | async-start | bytes 4194304 | tf_op jit(solution)/shard_map/all_to_all | solution.py:107
  17.1 48.2 %all-to-all-done = bf16[2,16,8,4096]{3,1,0,2:T(8,128)(2,1)S(1)} async-done(((bf16[2,16,8,4096]{3,1,0,2:T(8,128)(2,1)}), bf16[2,16,8,4096]{3,1,0,2:T(8,128)(2,1)S(1)}, u32[]{:S(2)}, u32[]{:S(2)}) %all-to-all-start) | async-done | bytes 2097184 | tf_op jit(solution)/shard_map/all_to_all | solution.py:107
  65.3 2.2 copy.94
  67.5 1.3 copy.139
  71.0 27.7 %all_to_all.56 = bf16[2,32,2,4096]{3,2,0,1:T(2,128)(2,1)S(1)} all-to-all(bf16[2,32,2,4096]{3,2,0,1:T(2,128)(2,1)S(1)} %copy.95), channel_id=1, replica_groups=mesh['chan'=4,'pulse'=4,'range'=2] {'chan'}, dimensions={1} | all-to-all | bytes 2097152 | tf_op jit(solution)/shard_map/all_to_all | solution.py:113
  100.6 6.4 %reshape.192 = f32[2,4096,2]{2,1,0:T(8,128)} reshape(f32[2,8192]{1,0:T(2,128)S(1)} %copy-done.1) | data formatting | bytes 131072 | tf_op jit(solution)/shard_map/reshape | solution.py:139
  107.0 4.7 %dynamic-slice_reduce_fusion = f32[2,4096]{1,0:T(2,128)S(1)} fusion(f32[2,4096,2]{2,1,0:T(8,128)} %reshape.192, s32[]{:T(128)S(6)} %select_n.134), kind=kLoop, calls=%fused_computation.31 | loop fusion | bytes 65540 | tf_op jit(solution)/shard_map/jit(dynamic_index_in_dim)/dynamic_slice | solution.py:140
  112.4 20.3 %all-gather.4.cloned.1.call-done = bf16[2,8,8,8192]{3,1,2,0:T(8,128)(2,1)} async-done(((bf16[2,8,8,4096]{3,1,2,0:T(8,128)(2,1)}), bf16[2,8,8,8192]{3,1,2,0:T(8,128)(2,1)}) %all-gather.4.cloned.1.call-update) | async-done | bytes 2097168 | tf_op jit(solution)/shard_map/all_gather | solution.py:119
  132.7 3.9 %fusion.286 = (f32[1,8,8,8192]{3,1,2,0:T(8,128)}, f32[1,8,8,8192]{3,1,2,0:T(8,128)}) fusion(bf16[2,8,8,8192]{3,1,2,0:T(8,128)(2,1)} %all-gather.4.cloned.1.call-done), kind=kLoop, calls=%fused_computation.385 | loop fusion | bytes 8388608 | tf_op jit(solution)/shard_map/slice | solution.py:130
  136.7 3.0 reshape.207
  139.7 4.2 %reshape.208 = f32[8,8,2,4096]{3,2,0,1:T(2,128)} reshape(f32[1,8,8,8192]{3,1,2,0:T(8,128)} %get-tuple-element.12) | data formatting | bytes 4194304 | tf_op jit(solution)/shard_map/squeeze | solution.py:130
  143.9 5.8 %subtract_reduce_fusion.1 = (f32[8,8,4096]{2,1,0:T(8,128)S(1)}, f32[8,8,4096]{2,1,0:T(8,128)S(1)}) fusion(f32[8,8,2,4096]{3,2,0,1:T(2,128)} %reshape.208, f32[8,8,2,4096]{3,2,0,1:T(2,128)S(1)} %reshape.207, f32[2]{0:T(128)S(1)} %get-tuple-element.30, f32[2]{0:T(128)S(1)} %get-tuple-element.29), kind=kLoop, calls=%fused_computation.35 | loop fusion | flops 3670016 | bytes 6291472 | tf_op jit(solution)/shard_map/reduce_sum | solution.py:130
  150.9 1.5 fusion.99
  152.4 1.5 fusion.100
  153.9 1.5 fusion.3
  155.4 1.5 fusion.2
  156.9 1.6 fusion.87
  168.4 1.4 fusion.91
  169.8 2.2 fusion.1
  172.0 2.4 reshape.194
  174.4 2.2 fusion
  176.5 1.5 reshape.195
  178.1 1.6 multiply_subtract_fusion
  180.5 32.5 %all-gather.6.cloned.1.call-done = f32[8,8,8192]{2,1,0:T(8,128)} async-done(((f32[8,8,4096]{2,1,0:T(8,128)}), f32[8,8,8192]{2,1,0:T(8,128)}) %all-gather.6.cloned.1.call-update) | async-done | bytes 2097168 | tf_op jit(solution)/shard_map/all_gather | solution.py:148
  212.9 34.7 %all-gather.8.cloned.1.call-done = f32[8,8,8192]{2,1,0:T(8,128)} async-done(((f32[8,8,4096]{2,1,0:T(8,128)}), f32[8,8,8192]{2,1,0:T(8,128)}) %all-gather.8.cloned.1.call-update) | async-done | bytes 2097168 | tf_op jit(solution)/shard_map/all_gather | solution.py:149
  247.6 3.2 subtract_reduce_fusion
  252.8 17.0 %all_to_all.57 = bf16[4,2,8,8,1024]{4,3,2,1,0:T(8,128)(2,1)S(1)} all-to-all(bf16[4,2,8,8,1024]{4,3,2,1,0:T(8,128)(2,1)S(1)} %copy.118), channel_id=1, replica_groups=mesh['chan'=4,'pulse'=4,'range'=2] {'pulse'}, dimensions={0} | all-to-all | bytes 2097152 | tf_op jit(solution)/shard_map/all_to_all | solution.py:168
  272.0 16.9 %all_to_all.58 = f32[8,32,1024]{2,0,1:T(8,128)S(1)} all-to-all(f32[8,32,1024]{2,0,1:T(8,128)S(1)} %copy.121), channel_id=1, replica_groups=mesh['chan'=4,'pulse'=4,'range'=2] {'pulse'}, dimensions={1} | all-to-all | bytes 2097152 | tf_op jit(solution)/shard_map/all_to_all | solution.py:179
  289.5 2.4 collective-permute-start
  293.5 4.2 %collective-permute-done.1 = f32[8,8,20]{2,1,0:T(8,128)S(1)} collective-permute-done((f32[8,8,20]{2,1,0:T(8,128)S(1)}, f32[8,8,20]{2,1,0:T(8,128)S(1)}, u32[]{:S(2)}, u32[]{:S(2)}) %collective-permute-start.1) | collective-permute-done | bytes 5152 | tf_op jit(solution)/shard_map/ppermute | solution.py:21
  297.7 12.2 %fusion.14 = f32[8,8,4096]{2,1,0:T(8,128)} fusion(f32[8,8,4096]{2,1,0:T(8,128)S(1)} %bitcast.152, f32[8,8,20]{2,1,0:T(8,128)S(1)} %collective-permute-done.1, f32[8,8,20]{2,1,0:T(8,128)S(1)} %collective-permute-done), kind=kLoop, calls=%fused_computation.66 | loop fusion | flops 17301504 | bytes 2107392 | tf_op jit(solution)/shard_map/div | solution.py:198
  (54 shorter events, 23.0 us)
Async XLA Ops:
  10.6 6.5 %copy-start.2 = (bf16[2,32,64]{2,1,0:T(8,128)(2,1)S(1)}, bf16[2,32,64]{2,1,0:T(8,128)(2,1)}, u32[]{:S(2)}) copy-start(bf16[2,32,64]{2,1,0:T(8,128)(2,1)} %param.4) | copy-start | bytes 24580
  10.6 54.7 %all-to-all-start = ((bf16[2,16,8,4096]{3,1,0,2:T(8,128)(2,1)}), bf16[2,16,8,4096]{3,1,0,2:T(8,128)(2,1)S(1)}, u32[]{:S(2)}, u32[]{:S(2)}) async-start(bf16[2,16,8,4096]{3,1,0,2:T(8,128)(2,1)} %copy.93), calls=%async_computation | async-start | bytes 4194304 | tf_op jit(solution)/shard_map/all_to_all | solution.py:107
  17.1 115.6 %all-gather.4.cloned.1.call-start = ((), (), s32[]{:S(2)}) async-start(), calls=%async_computation.4 | async-start | bytes 3145728 | tf_op jit(solution)/shard_map/all_gather | solution.py:119
  99.3 1.3 copy-start.1
  100.4 112.6 %all-gather.6.cloned.1.call-start = ((), (), s32[]{:S(2)}) async-start(), calls=%async_computation.5 | async-start | bytes 3145728 | tf_op jit(solution)/shard_map/all_gather | solution.py:148
  176.5 1.5 copy-start
  179.7 67.9 %all-gather.8.cloned.1.call-start = ((), (), s32[]{:S(2)}) async-start(), calls=%async_computation.6 | async-start | bytes 3145728 | tf_op jit(solution)/shard_map/all_gather | solution.py:149
  289.5 4.0 %collective-permute-start = (f32[8,8,20]{2,1,0:T(8,128)S(1)}, f32[8,8,20]{2,1,0:T(8,128)S(1)}, u32[]{:S(2)}, u32[]{:S(2)}) collective-permute-start(f32[8,8,20]{2,1,0:T(8,128)S(1)} %get-tuple-element.13), channel_id=1, source_target_pairs={{0,1},{2,3},{4,5},{6,7},{8,9},{10,11},{12,13},{14,15},{16,17},{18,... | collective-permute-start | bytes 15368 | tf_op jit(solution)/shard_map/ppermute | solution.py:20
  291.9 5.8 %collective-permute-start.1 = (f32[8,8,20]{2,1,0:T(8,128)S(1)}, f32[8,8,20]{2,1,0:T(8,128)S(1)}, u32[]{:S(2)}, u32[]{:S(2)}) collective-permute-start(f32[8,8,20]{2,1,0:T(8,128)S(1)} %get-tuple-element.14), channel_id=1, source_target_pairs={{1,0},{3,2},{5,4},{7,6},{9,8},{11,10},{13,12},{15,14},{17,16},{19,... | collective-permute-start | bytes 15368 | tf_op jit(solution)/shard_map/ppermute | solution.py:21
Sparse Core Ops, SparseCore 0:
  100.5 32.1 all-gather.3
  179.8 33.0 all-gather.5
  214.5 33.0 all-gather.7
